TPU v7x, 256 devices: a whole 4x4x8 slice. The times are simulated.
256 devices in a mesh: rel: 2 (over y_hi), row: 8 (over y_lo, x), col: 16 (over z, core).
Axes of the slice: x: 4, y: 4 (y_hi: 2, y_lo: 2; y = y_hi * 2 + y_lo), z: 8, core: 2. Of those that a mesh axis runs over, the one named last changes fastest.
Arguments:
- features: float32 [4, 128, 256, 128], P('rel', ('row', 'col')), may hold values from -6 to 6
- lap_tiles: bfloat16 [4, 8, 16, 16, 256, 256], P('rel', 'row', 'col'), may hold values from -0.046875 to 0.046875
- tile_rows: int32 [4, 8, 16, 16], P('rel', 'row', 'col'), may hold values from 0 to 15
- tile_cols: int32 [4, 8, 16, 16], P('rel', 'row', 'col'), may hold values from 0 to 7
- tile_count: int32 [4, 8, 16], P('rel', 'row', 'col'), may hold values from 2 to 16, as said below
- cheb_coefs: float32 [4, 5], P('rel'), may hold values from -1 to 1
- merging_weight: bfloat16 [512, 128], replicated, may hold values from -0.25 to 0.25
Outputs:
- merged_rows: float32 [128, 256, 128], P(('row', 'col'), 'rel')
Inputs may be any that keep to these rules, and one draw needn't show every extreme that they name: Only the first tile_count slots of a device count; in every relation some device has 16 valid slots.
All inputs are finite; a program needn't handle non-finite values.
Results may differ from a plain program's by a relative error of at most 0.0063.
Values may be sent and summed in bfloat16 or wider, within the bound.
A program may use at most 64 MiB of HBM per device.

v0:
```python
import jax
import jax.numpy as jnp
from jax import lax
from jax.sharding import PartitionSpec as P

ORDERS = 4


def sent_to_all(x, axis):
    count = lax.axis_size(axis)
    return lax.all_to_all(jnp.broadcast_to(x[None], (count, *x.shape)), axis, 0, 0, tiled=True)


def laid_out(pieces, dim):
    pieces = jnp.moveaxis(pieces, 0, dim)
    dims = pieces.shape
    return pieces.reshape(*dims[:dim], dims[dim] * dims[dim + 1], *dims[dim + 2 :])


def gather_directly(x, axis, dim):
    pieces = sent_to_all(x, axis)
    return laid_out(pieces, dim)


def cut_along(x, dim, count):
    dims = x.shape
    pieces = x.reshape(*dims[:dim], count, dims[dim] // count, *dims[dim + 1 :])
    return jnp.moveaxis(pieces, dim, 0)


def sum_at_owner(x, axis, dim):
    pieces = cut_along(x, dim, lax.axis_size(axis))
    arrived = lax.all_to_all(pieces, axis, split_axis=0, concat_axis=0, tiled=True)
    return arrived.astype(jnp.float32).sum(axis=0)


def local_product(block_tiles, block_rows, block_cols, block_count, source, col_count, piece_rows):
    tile_size = block_tiles.shape[-1]
    width = source.shape[-1]
    running = jnp.zeros((col_count * piece_rows, width), jnp.float32)

    def advance(slot_index, running):
        block_tile = block_tiles[slot_index]
        start_col = block_cols[slot_index] * tile_size
        start_row = block_rows[slot_index] * tile_size
        source_rows = lax.dynamic_slice_in_dim(source, start_col, tile_size, 0)
        product = jnp.dot(block_tile, source_rows, preferred_element_type=jnp.float32)
        current = lax.dynamic_slice_in_dim(running, start_row, tile_size, 0)
        return lax.dynamic_update_slice_in_dim(running, current + product, start_row, 0)

    running = lax.fori_loop(0, block_count, advance, running)
    return running.reshape(col_count, piece_rows, width)


def local(features, lap_tiles, tile_rows, tile_cols, tile_count, cheb_coefs, merging_weight):
    col_count = lax.axis_size("col")
    rel_count = lax.axis_size("rel")
    local_rels = features.shape[0]
    piece_rows = features.shape[2]
    width = features.shape[3]
    current = features
    earlier = current
    embedding = cheb_coefs[:, 0][:, None, None, None] * current
    for degree in range(1, ORDERS + 1):
        operand = current.astype(jnp.bfloat16)
        collected = []
        for relation in range(local_rels):
            gathered = gather_directly(operand[relation], "row", 0)
            partial_value = local_product(
                lap_tiles[relation, 0, 0],
                tile_rows[relation, 0, 0],
                tile_cols[relation, 0, 0],
                tile_count[relation, 0, 0],
                gathered.reshape(-1, width),
                col_count,
                piece_rows,
            )
            collected.append(sum_at_owner(partial_value.astype(jnp.bfloat16), "col", 0))
        applied = jnp.stack(collected)
        if degree == 1:
            following = applied
        else:
            following = 2.0 * applied - earlier
        earlier, current = (current, following)
        embedding = embedding + cheb_coefs[:, degree][:, None, None, None] * current
    embedded = embedding.astype(jnp.bfloat16)
    exchanged = lax.all_to_all(embedded, "rel", split_axis=2, concat_axis=3, tiled=True)
    grouped = merging_weight.reshape(rel_count, local_rels, width, width)
    merged_rows = jnp.zeros((exchanged.shape[2], width), jnp.float32)
    for relation in range(local_rels):
        weight_rows = grouped[:, relation].reshape(rel_count * width, width)
        merged_rows = merged_rows + jnp.dot(
            exchanged[relation, 0], weight_rows, preferred_element_type=jnp.float32
        )
    return merged_rows[None]


def solution(mesh):
    placed = (
        P("rel", ("row", "col"), None, None),
        P("rel", "row", "col", None, None, None),
        P("rel", "row", "col", None),
        P("rel", "row", "col", None),
        P("rel", "row", "col"),
        P("rel", None),
        P(),
    )
    return jax.shard_map(
        local, mesh=mesh, in_specs=placed, out_specs=P(("row", "col"), "rel", None), check_vma=False
    )
```

profile of v0, /device:TPU:1, one launch (start us, length us, event | category | flops | bytes accessed | tf_op | source)
XLA Modules:
  0.0 811.1 jit_solution(12106921629094762146)
XLA Ops:
  1.9 5.9 all-to-all-start
  22.5 34.4 %while.80 = (s32[]{:T(128)}, f32[4096,128]{1,0:T(8,128)S(1)}, s32[]{:T(128)}, s32[16]{0:T(128)S(1)}, bf16[16,256,256]{2,1,0:T(8,128)(2,1)}, /*index=5*/s32[16]{0...) while((s32[]{:T(128)}, f32[4096,128]{1,0:T(8,128)S(1)}, ...), condition=%wide.region_1.0_spmd, body=%wide.region_0.0_spmd.sunk | while | flops 16809996 | bytes 459039 | solution.py:51
  58.1 43.0 %all-to-all-start.1 = ((bf16[16,1,256,128]{3,2,1,0:T(8,128)(2,1)}), bf16[16,1,256,128]{3,2,1,0:T(8,128)(2,1)S(1)}, u32[]{:S(2)}, u32[]{:S(2)}) async-start(bf16[16,1,256,128]{3,2,1,0:T(8,128)(2,1)} %bitcast.30), calls=%async_computation.1 | async-start | bytes 2097152 | tf_op jit(solution)/shard_map/all_to_all | solution.py:33
  101.3 9.1 %while.81 = (s32[]{:T(128)}, f32[4096,128]{1,0:T(8,128)S(1)}, s32[]{:T(128)}, s32[16]{0:T(128)S(1)}, bf16[16,256,256]{2,1,0:T(8,128)(2,1)}, /*index=5*/s32[16]{0...) while((s32[]{:T(128)}, f32[4096,128]{1,0:T(8,128)S(1)}, ...), condition=%wide.region_4.0_spmd, body=%wide.region_3.0_spmd.sunk | while | flops 16809996 | bytes 459039 | solution.py:51
  111.5 17.6 %all-to-all-done.1 = bf16[16,1,256,128]{3,2,1,0:T(8,128)(2,1)S(1)} async-done(((bf16[16,1,256,128]{3,2,1,0:T(8,128)(2,1)}), bf16[16,1,256,128]{3,2,1,0:T(8,128)(2,1)S(1)}, u32[]{:S(2)}, u32[]{:S(2)}) %all-to-all-start.1) | async-done | bytes 1048608 | tf_op jit(solution)/shard_map/all_to_all | solution.py:33
  129.1 46.5 %all-to-all-start.3 = ((bf16[16,1,256,128]{3,2,1,0:T(8,128)(2,1)}), bf16[16,1,256,128]{3,2,1,0:T(8,128)(2,1)S(1)}, u32[]{:S(2)}, u32[]{:S(2)}) async-start(bf16[16,1,256,128]{3,2,1,0:T(8,128)(2,1)} %bitcast.38), calls=%async_computation.3 | async-start | bytes 2097152 | tf_op jit(solution)/shard_map/all_to_all | solution.py:33
  175.7 27.8 %all-to-all-done.3 = bf16[16,1,256,128]{3,2,1,0:T(8,128)(2,1)S(1)} async-done(((bf16[16,1,256,128]{3,2,1,0:T(8,128)(2,1)}), bf16[16,1,256,128]{3,2,1,0:T(8,128)(2,1)S(1)}, u32[]{:S(2)}, u32[]{:S(2)}) %all-to-all-start.3) | async-done | bytes 1048608 | tf_op jit(solution)/shard_map/all_to_all | solution.py:33
  204.7 6.1 all-to-all-start.4
  210.7 9.7 %all-to-all-done.4 = bf16[8,1,256,128]{3,2,1,0:T(8,128)(2,1)S(1)} async-done(((bf16[8,1,256,128]{3,2,1,0:T(8,128)(2,1)}), bf16[8,1,256,128]{3,2,1,0:T(8,128)(2,1)S(1)}, u32[]{:S(2)}, u32[]{:S(2)}) %all-to-all-start.4) | async-done | bytes 524320 | tf_op jit(solution)/shard_map/all_to_all | solution.py:11
  225.0 32.5 %while.82 = (s32[]{:T(128)}, f32[4096,128]{1,0:T(8,128)S(1)}, s32[]{:T(128)}, s32[16]{0:T(128)S(1)}, bf16[16,256,256]{2,1,0:T(8,128)(2,1)}, /*index=5*/s32[16]{0...) while((s32[]{:T(128)}, f32[4096,128]{1,0:T(8,128)S(1)}, ...), condition=%wide.region_7.0_spmd, body=%wide.region_6.0_spmd.sunk | while | flops 16809996 | bytes 459039 | solution.py:51
  258.6 36.2 %all-to-all-start.5 = ((bf16[16,1,256,128]{3,2,1,0:T(8,128)(2,1)}), bf16[16,1,256,128]{3,2,1,0:T(8,128)(2,1)S(1)}, u32[]{:S(2)}, u32[]{:S(2)}) async-start(bf16[16,1,256,128]{3,2,1,0:T(8,128)(2,1)} %bitcast.42), calls=%async_computation.5 | async-start | bytes 2097152 | tf_op jit(solution)/shard_map/all_to_all | solution.py:33
  294.9 9.2 %while.83 = (s32[]{:T(128)}, f32[4096,128]{1,0:T(8,128)S(1)}, s32[]{:T(128)}, s32[16]{0:T(128)S(1)}, bf16[16,256,256]{2,1,0:T(8,128)(2,1)}, /*index=5*/s32[16]{0...) while((s32[]{:T(128)}, f32[4096,128]{1,0:T(8,128)S(1)}, ...), condition=%wide.region_10.0_spmd, body=%wide.region_9.0_spmd.sunk | while | flops 16809996 | bytes 459039 | solution.py:51
  305.2 17.5 %all-to-all-done.5 = bf16[16,1,256,128]{3,2,1,0:T(8,128)(2,1)S(1)} async-done(((bf16[16,1,256,128]{3,2,1,0:T(8,128)(2,1)}), bf16[16,1,256,128]{3,2,1,0:T(8,128)(2,1)S(1)}, u32[]{:S(2)}, u32[]{:S(2)}) %all-to-all-start.5) | async-done | bytes 1048608 | tf_op jit(solution)/shard_map/all_to_all | solution.py:33
  322.7 47.4 %all-to-all-start.7 = ((bf16[16,1,256,128]{3,2,1,0:T(8,128)(2,1)}), bf16[16,1,256,128]{3,2,1,0:T(8,128)(2,1)S(1)}, u32[]{:S(2)}, u32[]{:S(2)}) async-start(bf16[16,1,256,128]{3,2,1,0:T(8,128)(2,1)} %bitcast.46), calls=%async_computation.7 | async-start | bytes 2097152 | tf_op jit(solution)/shard_map/all_to_all | solution.py:33
  370.3 27.8 %all-to-all-done.7 = bf16[16,1,256,128]{3,2,1,0:T(8,128)(2,1)S(1)} async-done(((bf16[16,1,256,128]{3,2,1,0:T(8,128)(2,1)}), bf16[16,1,256,128]{3,2,1,0:T(8,128)(2,1)S(1)}, u32[]{:S(2)}, u32[]{:S(2)}) %all-to-all-start.7) | async-done | bytes 1048608 | tf_op jit(solution)/shard_map/all_to_all | solution.py:33
  399.2 7.9 all-to-all-start.8
  407.2 9.7 %all-to-all-done.8 = bf16[8,1,256,128]{3,2,1,0:T(8,128)(2,1)S(1)} async-done(((bf16[8,1,256,128]{3,2,1,0:T(8,128)(2,1)}), bf16[8,1,256,128]{3,2,1,0:T(8,128)(2,1)S(1)}, u32[]{:S(2)}, u32[]{:S(2)}) %all-to-all-start.8) | async-done | bytes 524320 | tf_op jit(solution)/shard_map/all_to_all | solution.py:11
  421.4 34.4 %while.84 = (s32[]{:T(128)}, f32[4096,128]{1,0:T(8,128)S(1)}, s32[]{:T(128)}, s32[16]{0:T(128)S(1)}, bf16[16,256,256]{2,1,0:T(8,128)(2,1)}, /*index=5*/s32[16]{0...) while((s32[]{:T(128)}, f32[4096,128]{1,0:T(8,128)S(1)}, ...), condition=%wide.region_13.0_spmd, body=%wide.region_12.0_spmd.sunk | while | flops 16809996 | bytes 459039 | solution.py:51
  457.0 38.1 %all-to-all-start.9 = ((bf16[16,1,256,128]{3,2,1,0:T(8,128)(2,1)}), bf16[16,1,256,128]{3,2,1,0:T(8,128)(2,1)S(1)}, u32[]{:S(2)}, u32[]{:S(2)}) async-start(bf16[16,1,256,128]{3,2,1,0:T(8,128)(2,1)} %bitcast.50), calls=%async_computation.9 | async-start | bytes 2097152 | tf_op jit(solution)/shard_map/all_to_all | solution.py:33
  495.2 9.1 %while.85 = (s32[]{:T(128)}, f32[4096,128]{1,0:T(8,128)S(1)}, s32[]{:T(128)}, s32[16]{0:T(128)S(1)}, bf16[16,256,256]{2,1,0:T(8,128)(2,1)}, /*index=5*/s32[16]{0...) while((s32[]{:T(128)}, f32[4096,128]{1,0:T(8,128)S(1)}, ...), condition=%wide.region_16.0_spmd, body=%wide.region_15.0_spmd.sunk | while | flops 16809996 | bytes 459039 | solution.py:51
  505.5 17.6 %all-to-all-done.9 = bf16[16,1,256,128]{3,2,1,0:T(8,128)(2,1)S(1)} async-done(((bf16[16,1,256,128]{3,2,1,0:T(8,128)(2,1)}), bf16[16,1,256,128]{3,2,1,0:T(8,128)(2,1)S(1)}, u32[]{:S(2)}, u32[]{:S(2)}) %all-to-all-start.9) | async-done | bytes 1048608 | tf_op jit(solution)/shard_map/all_to_all | solution.py:33
  523.1 46.6 %all-to-all-start.11 = ((bf16[16,1,256,128]{3,2,1,0:T(8,128)(2,1)}), bf16[16,1,256,128]{3,2,1,0:T(8,128)(2,1)S(1)}, u32[]{:S(2)}, u32[]{:S(2)}) async-start(bf16[16,1,256,128]{3,2,1,0:T(8,128)(2,1)} %bitcast.54), calls=%async_computation.11 | async-start | bytes 2097152 | tf_op jit(solution)/shard_map/all_to_all | solution.py:33
  569.8 27.8 %all-to-all-done.11 = bf16[16,1,256,128]{3,2,1,0:T(8,128)(2,1)S(1)} async-done(((bf16[16,1,256,128]{3,2,1,0:T(8,128)(2,1)}), bf16[16,1,256,128]{3,2,1,0:T(8,128)(2,1)S(1)}, u32[]{:S(2)}, u32[]{:S(2)}) %all-to-all-start.11) | async-done | bytes 1048608 | tf_op jit(solution)/shard_map/all_to_all | solution.py:33
  598.8 7.9 all-to-all-start.12
  606.7 9.7 %all-to-all-done.12 = bf16[8,1,256,128]{3,2,1,0:T(8,128)(2,1)S(1)} async-done(((bf16[8,1,256,128]{3,2,1,0:T(8,128)(2,1)}), bf16[8,1,256,128]{3,2,1,0:T(8,128)(2,1)S(1)}, u32[]{:S(2)}, u32[]{:S(2)}) %all-to-all-start.12) | async-done | bytes 524320 | tf_op jit(solution)/shard_map/all_to_all | solution.py:11
  621.0 36.6 %while.86 = (s32[]{:T(128)}, f32[4096,128]{1,0:T(8,128)S(1)}, s32[]{:T(128)}, s32[16]{0:T(128)S(1)}, bf16[16,256,256]{2,1,0:T(8,128)(2,1)}, /*index=5*/s32[16]{0...) while((s32[]{:T(128)}, f32[4096,128]{1,0:T(8,128)S(1)}, ...), condition=%wide.region_19.0_spmd, body=%wide.region_18.0_spmd.sunk | while | flops 16809996 | bytes 459039 | solution.py:51
  658.6 40.3 %all-to-all-start.13 = ((bf16[16,1,256,128]{3,2,1,0:T(8,128)(2,1)}), bf16[16,1,256,128]{3,2,1,0:T(8,128)(2,1)S(1)}, u32[]{:S(2)}, u32[]{:S(2)}) async-start(bf16[16,1,256,128]{3,2,1,0:T(8,128)(2,1)} %bitcast.58), calls=%async_computation.13 | async-start | bytes 2097152 | tf_op jit(solution)/shard_map/all_to_all | solution.py:33
  699.1 8.7 %while.87 = (s32[]{:T(128)}, f32[4096,128]{1,0:T(8,128)S(1)}, s32[]{:T(128)}, s32[16]{0:T(128)S(1)}, bf16[16,256,256]{2,1,0:T(8,128)(2,1)}, /*index=5*/s32[16]{0...) while((s32[]{:T(128)}, f32[4096,128]{1,0:T(8,128)S(1)}, ...), condition=%wide.region_22.0_spmd, body=%wide.region_21.0_spmd.sunk | while | flops 16809996 | bytes 459039 | solution.py:51
  708.9 18.0 %all-to-all-done.13 = bf16[16,1,256,128]{3,2,1,0:T(8,128)(2,1)S(1)} async-done(((bf16[16,1,256,128]{3,2,1,0:T(8,128)(2,1)}), bf16[16,1,256,128]{3,2,1,0:T(8,128)(2,1)S(1)}, u32[]{:S(2)}, u32[]{:S(2)}) %all-to-all-start.13) | async-done | bytes 1048608 | tf_op jit(solution)/shard_map/all_to_all | solution.py:33
  727.0 43.4 %all-to-all-start.15 = ((bf16[16,1,256,128]{3,2,1,0:T(8,128)(2,1)}), bf16[16,1,256,128]{3,2,1,0:T(8,128)(2,1)S(1)}, u32[]{:S(2)}, u32[]{:S(2)}) async-start(bf16[16,1,256,128]{3,2,1,0:T(8,128)(2,1)} %bitcast.62), calls=%async_computation.15 | async-start | bytes 2097152 | tf_op jit(solution)/shard_map/all_to_all | solution.py:33
  770.7 27.6 %all-to-all-done.15 = bf16[16,1,256,128]{3,2,1,0:T(8,128)(2,1)S(1)} async-done(((bf16[16,1,256,128]{3,2,1,0:T(8,128)(2,1)}), bf16[16,1,256,128]{3,2,1,0:T(8,128)(2,1)S(1)}, u32[]{:S(2)}, u32[]{:S(2)}) %all-to-all-start.15) | async-done | bytes 1048608 | tf_op jit(solution)/shard_map/all_to_all | solution.py:33
  799.5 5.4 all-to-all-start.16
  (225 shorter events, 143.3 us)
Async XLA Ops:
  1.9 16.1 %all-to-all-start = ((bf16[8,1,256,128]{3,2,1,0:T(8,128)(2,1)}), bf16[8,1,256,128]{3,2,1,0:T(8,128)(2,1)S(1)}, u32[]{:S(2)}, u32[]{:S(2)}) async-start(bf16[8,1,256,128]{3,2,1,0:T(8,128)(2,1)} %broadcast_in_dim.60), calls=%async_computation | async-start | bytes 1048576 | tf_op jit(solution)/shard_map/all_to_all | solution.py:11
  18.9 39.2 %all-to-all-start.2 = ((bf16[8,1,256,128]{3,2,1,0:T(8,128)(2,1)}), bf16[8,1,256,128]{3,2,1,0:T(8,128)(2,1)S(1)}, u32[]{:S(2)}, u32[]{:S(2)}) async-start(bf16[8,1,256,128]{3,2,1,0:T(8,128)(2,1)} %broadcast_in_dim.62), calls=%async_computation.2 | async-start | bytes 1048576 | tf_op jit(solution)/shard_map/all_to_all | solution.py:11
  58.1 43.0 %copy-start.5 = (bf16[8,1,256,128]{3,2,1,0:T(8,128)(2,1)}, bf16[8,1,256,128]{3,2,1,0:T(8,128)(2,1)S(1)}, u32[]{:S(2)}) copy-start(bf16[8,1,256,128]{3,2,1,0:T(8,128)(2,1)S(1)} %all-to-all-done.2) | copy-start | bytes 1572868
  58.1 71.0 %all-to-all-start.1 = ((bf16[16,1,256,128]{3,2,1,0:T(8,128)(2,1)}), bf16[16,1,256,128]{3,2,1,0:T(8,128)(2,1)S(1)}, u32[]{:S(2)}, u32[]{:S(2)}) async-start(bf16[16,1,256,128]{3,2,1,0:T(8,128)(2,1)} %bitcast.30), calls=%async_computation.1 | async-start | bytes 2097152 | tf_op jit(solution)/shard_map/all_to_all | solution.py:33
  129.1 74.5 %all-to-all-start.3 = ((bf16[16,1,256,128]{3,2,1,0:T(8,128)(2,1)}), bf16[16,1,256,128]{3,2,1,0:T(8,128)(2,1)S(1)}, u32[]{:S(2)}, u32[]{:S(2)}) async-start(bf16[16,1,256,128]{3,2,1,0:T(8,128)(2,1)} %bitcast.38), calls=%async_computation.3 | async-start | bytes 2097152 | tf_op jit(solution)/shard_map/all_to_all | solution.py:33
  204.7 15.8 %all-to-all-start.4 = ((bf16[8,1,256,128]{3,2,1,0:T(8,128)(2,1)}), bf16[8,1,256,128]{3,2,1,0:T(8,128)(2,1)S(1)}, u32[]{:S(2)}, u32[]{:S(2)}) async-start(bf16[8,1,256,128]{3,2,1,0:T(8,128)(2,1)} %broadcast_in_dim.64), calls=%async_computation.4 | async-start | bytes 1048576 | tf_op jit(solution)/shard_map/all_to_all | solution.py:11
  221.3 37.3 %all-to-all-start.6 = ((bf16[8,1,256,128]{3,2,1,0:T(8,128)(2,1)}), bf16[8,1,256,128]{3,2,1,0:T(8,128)(2,1)S(1)}, u32[]{:S(2)}, u32[]{:S(2)}) async-start(bf16[8,1,256,128]{3,2,1,0:T(8,128)(2,1)} %broadcast_in_dim.66), calls=%async_computation.6 | async-start | bytes 1048576 | tf_op jit(solution)/shard_map/all_to_all | solution.py:11
  258.6 36.2 %copy-start.6 = (bf16[8,1,256,128]{3,2,1,0:T(8,128)(2,1)}, bf16[8,1,256,128]{3,2,1,0:T(8,128)(2,1)S(1)}, u32[]{:S(2)}) copy-start(bf16[8,1,256,128]{3,2,1,0:T(8,128)(2,1)S(1)} %all-to-all-done.6) | copy-start | bytes 1572868
  258.6 64.2 %all-to-all-start.5 = ((bf16[16,1,256,128]{3,2,1,0:T(8,128)(2,1)}), bf16[16,1,256,128]{3,2,1,0:T(8,128)(2,1)S(1)}, u32[]{:S(2)}, u32[]{:S(2)}) async-start(bf16[16,1,256,128]{3,2,1,0:T(8,128)(2,1)} %bitcast.42), calls=%async_computation.5 | async-start | bytes 2097152 | tf_op jit(solution)/shard_map/all_to_all | solution.py:33
  322.7 75.6 %copy-start = (f32[2,1,256,128]{3,2,1,0:T(8,128)S(1)}, f32[2,1,256,128]{3,2,1,0:T(8,128)}, u32[]{:S(2)}) copy-start(f32[2,1,256,128]{3,2,1,0:T(8,128)} %param.23) | copy-start | bytes 786436
  322.7 75.4 %all-to-all-start.7 = ((bf16[16,1,256,128]{3,2,1,0:T(8,128)(2,1)}), bf16[16,1,256,128]{3,2,1,0:T(8,128)(2,1)S(1)}, u32[]{:S(2)}, u32[]{:S(2)}) async-start(bf16[16,1,256,128]{3,2,1,0:T(8,128)(2,1)} %bitcast.46), calls=%async_computation.7 | async-start | bytes 2097152 | tf_op jit(solution)/shard_map/all_to_all | solution.py:33
  370.3 47.5 %copy-start.8 = (f32[256,128]{1,0:T(8,128)}, f32[256,128]{1,0:T(8,128)S(1)}, u32[]{:S(2)}) copy-start(f32[256,128]{1,0:T(8,128)S(1)} %convert_reduce_fusion.5) | copy-start | bytes 393220
  399.2 17.6 %all-to-all-start.8 = ((bf16[8,1,256,128]{3,2,1,0:T(8,128)(2,1)}), bf16[8,1,256,128]{3,2,1,0:T(8,128)(2,1)S(1)}, u32[]{:S(2)}, u32[]{:S(2)}) async-start(bf16[8,1,256,128]{3,2,1,0:T(8,128)(2,1)} %broadcast_in_dim.68), calls=%async_computation.8 | async-start | bytes 1048576 | tf_op jit(solution)/shard_map/all_to_all | solution.py:11
  417.7 39.2 %all-to-all-start.10 = ((bf16[8,1,256,128]{3,2,1,0:T(8,128)(2,1)}), bf16[8,1,256,128]{3,2,1,0:T(8,128)(2,1)S(1)}, u32[]{:S(2)}, u32[]{:S(2)}) async-start(bf16[8,1,256,128]{3,2,1,0:T(8,128)(2,1)} %broadcast_in_dim.70), calls=%async_computation.10 | async-start | bytes 1048576 | tf_op jit(solution)/shard_map/all_to_all | solution.py:11
  457.0 38.1 %copy-start.7 = (bf16[8,1,256,128]{3,2,1,0:T(8,128)(2,1)}, bf16[8,1,256,128]{3,2,1,0:T(8,128)(2,1)S(1)}, u32[]{:S(2)}) copy-start(bf16[8,1,256,128]{3,2,1,0:T(8,128)(2,1)S(1)} %all-to-all-done.10) | copy-start | bytes 1572868
  457.0 66.1 %all-to-all-start.9 = ((bf16[16,1,256,128]{3,2,1,0:T(8,128)(2,1)}), bf16[16,1,256,128]{3,2,1,0:T(8,128)(2,1)S(1)}, u32[]{:S(2)}, u32[]{:S(2)}) async-start(bf16[16,1,256,128]{3,2,1,0:T(8,128)(2,1)} %bitcast.50), calls=%async_computation.9 | async-start | bytes 2097152 | tf_op jit(solution)/shard_map/all_to_all | solution.py:33
  523.1 74.7 %copy-start.2 = (f32[256,128]{1,0:T(8,128)S(1)}, f32[256,128]{1,0:T(8,128)}, u32[]{:S(2)}) copy-start(f32[256,128]{1,0:T(8,128)} %copy-done.1) | copy-start | bytes 393220
  523.1 74.6 %all-to-all-start.11 = ((bf16[16,1,256,128]{3,2,1,0:T(8,128)(2,1)}), bf16[16,1,256,128]{3,2,1,0:T(8,128)(2,1)S(1)}, u32[]{:S(2)}, u32[]{:S(2)}) async-start(bf16[16,1,256,128]{3,2,1,0:T(8,128)(2,1)} %bitcast.54), calls=%async_computation.11 | async-start | bytes 2097152 | tf_op jit(solution)/shard_map/all_to_all | solution.py:33
  569.8 47.5 %copy-start.12 = (f32[256,128]{1,0:T(8,128)}, f32[256,128]{1,0:T(8,128)S(1)}, u32[]{:S(2)}) copy-start(f32[256,128]{1,0:T(8,128)S(1)} %convert_reduce_fusion.3) | copy-start | bytes 393220
  598.8 17.6 %all-to-all-start.12 = ((bf16[8,1,256,128]{3,2,1,0:T(8,128)(2,1)}), bf16[8,1,256,128]{3,2,1,0:T(8,128)(2,1)S(1)}, u32[]{:S(2)}, u32[]{:S(2)}) async-start(bf16[8,1,256,128]{3,2,1,0:T(8,128)(2,1)} %broadcast_in_dim.72), calls=%async_computation.12 | async-start | bytes 1048576 | tf_op jit(solution)/shard_map/all_to_all | solution.py:11
  617.3 41.3 %all-to-all-start.14 = ((bf16[8,1,256,128]{3,2,1,0:T(8,128)(2,1)}), bf16[8,1,256,128]{3,2,1,0:T(8,128)(2,1)S(1)}, u32[]{:S(2)}, u32[]{:S(2)}) async-start(bf16[8,1,256,128]{3,2,1,0:T(8,128)(2,1)} %broadcast_in_dim.74), calls=%async_computation.14 | async-start | bytes 1048576 | tf_op jit(solution)/shard_map/all_to_all | solution.py:11
  658.6 40.3 %copy-start.4 = (bf16[8,1,256,128]{3,2,1,0:T(8,128)(2,1)}, bf16[8,1,256,128]{3,2,1,0:T(8,128)(2,1)S(1)}, u32[]{:S(2)}) copy-start(bf16[8,1,256,128]{3,2,1,0:T(8,128)(2,1)S(1)} %all-to-all-done.14) | copy-start | bytes 1572868
  658.6 68.3 %all-to-all-start.13 = ((bf16[16,1,256,128]{3,2,1,0:T(8,128)(2,1)}), bf16[16,1,256,128]{3,2,1,0:T(8,128)(2,1)S(1)}, u32[]{:S(2)}, u32[]{:S(2)}) async-start(bf16[16,1,256,128]{3,2,1,0:T(8,128)(2,1)} %bitcast.58), calls=%async_computation.13 | async-start | bytes 2097152 | tf_op jit(solution)/shard_map/all_to_all | solution.py:33
  707.8 62.5 %copy-start.17 = (f32[2,5]{1,0:T(2,128)S(1)}, f32[2,5]{1,0:T(2,128)}, u32[]{:S(2)}) copy-start(f32[2,5]{1,0:T(2,128)} %param.28) | copy-start | bytes 124
  726.9 71.5 %copy-start.3 = (f32[256,128]{1,0:T(8,128)S(1)}, f32[256,128]{1,0:T(8,128)}, u32[]{:S(2)}) copy-start(f32[256,128]{1,0:T(8,128)} %copy-done.1) | copy-start | bytes 393220
  727.0 71.6 %copy-start.9 = (f32[256,128]{1,0:T(8,128)S(1)}, f32[256,128]{1,0:T(8,128)}, u32[]{:S(2)}) copy-start(f32[256,128]{1,0:T(8,128)} %copy-done.8) | copy-start | bytes 393220
  727.0 71.6 %copy-start.11 = (f32[256,128]{1,0:T(8,128)S(1)}, f32[256,128]{1,0:T(8,128)}, u32[]{:S(2)}) copy-start(f32[256,128]{1,0:T(8,128)} %copy-done.10) | copy-start | bytes 393220
  727.0 71.6 %copy-start.13 = (f32[256,128]{1,0:T(8,128)S(1)}, f32[256,128]{1,0:T(8,128)}, u32[]{:S(2)}) copy-start(f32[256,128]{1,0:T(8,128)} %copy-done.12) | copy-start | bytes 393220
  727.0 71.6 %copy-start.15 = (f32[256,128]{1,0:T(8,128)S(1)}, f32[256,128]{1,0:T(8,128)}, u32[]{:S(2)}) copy-start(f32[256,128]{1,0:T(8,128)} %copy-done.14) | copy-start | bytes 393220
  727.0 71.4 %all-to-all-start.15 = ((bf16[16,1,256,128]{3,2,1,0:T(8,128)(2,1)}), bf16[16,1,256,128]{3,2,1,0:T(8,128)(2,1)S(1)}, u32[]{:S(2)}, u32[]{:S(2)}) async-start(bf16[16,1,256,128]{3,2,1,0:T(8,128)(2,1)} %bitcast.62), calls=%async_computation.15 | async-start | bytes 2097152 | tf_op jit(solution)/shard_map/all_to_all | solution.py:33
  770.6 34.4 %copy-start.16 = (bf16[512,128]{1,0:T(8,128)(2,1)S(1)}, bf16[512,128]{1,0:T(8,128)(2,1)}, u32[]{:S(2)}) copy-start(bf16[512,128]{1,0:T(8,128)(2,1)} %param.29) | copy-start | bytes 393220
  799.5 10.3 %all-to-all-start.16 = ((bf16[2,1,256,128]{3,0,1,2:T(2,128)(2,1)}), bf16[2,1,256,128]{3,0,1,2:T(2,128)(2,1)S(1)}, u32[]{:S(2)}, u32[]{:S(2)}) async-start(bf16[2,1,256,128]{3,0,1,2:T(2,128)(2,1)} %copy.17), calls=%async_computation.16 | async-start | bytes 262144 | tf_op jit(solution)/shard_map/all_to_all | solution.py:87
  (6 other events, 83.4 us)
where the time goes:
time: 820 us; the launch traced here: 811 us
  starting transfers between devices  389 us (47%)
  waiting for transfers between devices  221 us (27%)
  loops' own time  81.7 us (10%)
  local copies, waits for them, and re-layouts  63.9 us (8%)
  matrix products  44.3 us (5%)
  other arithmetic  11.3 us (1%)
    all_to_all x8, starting transfers between devices, sum_at_owner(): lax.all_to_all(pieces, axis, split_axis=0, concat_axis=0, tiled=True)  342 us
    all_to_all x8, waiting for transfers between devices, sum_at_owner(): lax.all_to_all(pieces, axis, split_axis=0, concat_axis=0, tiled=True)  182 us
    another operation x8, loops' own time, local_product(): running = lax.fori_loop(0, block_count, advance, running)  81.7 us
    dot_general x40, matrix products, advance(): jnp.dot(block_tile, source_rows, preferred_element_type=jnp.float32)  43.3 us
    all_to_all x8, starting transfers between devices, sent_to_all(): lax.all_to_all(jnp.broadcast_to(x[None], (count, *x.shape)), axis, 0, 0,...  41.8 us
    all_to_all x8, waiting for transfers between devices, sent_to_all(): lax.all_to_all(jnp.broadcast_to(x[None], (count, *x.shape)), axis, 0, 0,...  34 us
    dynamic_slice x40, local copies, waits for them, and re-layouts, advance(): start_row = block_rows[slot_index] * tile_size  24.6 us
    dynamic_slice x40, local copies, waits for them, and re-layouts, advance(): start_col = block_cols[slot_index] * tile_size  24.5 us
  transfers between devices with their start and end apart: 17, of which 13 were waited for; matrix products, arithmetic and copies ran while one was open for 13% of the time, Pallas kernels for 0%

commit v1 on v0

v1 whole, which is shorter than its diff:
```python
import functools

import jax
import jax.numpy as jnp
from jax import lax
from jax.experimental import pallas as pl
from jax.experimental.pallas import tpu as pltpu
from jax.sharding import PartitionSpec as P

ORDERS = 4
X_CHIPS = 4
Y_LOW = 2
MESH = pl.DeviceIdType.MESH
ROW_OFFSETS = ((1, 2), (1, 1), (1, 3), (0, 2), (1, 0), (0, 1), (0, 3))
DELTAS = (4, 3, -3, 2, -2, 1, -1, 0)
MIDDLE = 3


def kernel(
    sizes,
    feats,
    tiles,
    rows,
    cols,
    count,
    coefs,
    weight,
    out,
    tiles_v,
    prefix,
    before,
    final,
    hist,
    emb,
    emb_send,
    emb_recv,
    load_sem,
    row_send,
    row_recv,
    pair_send,
    pair_recv,
    ring_send,
    ring_recv,
    rel_send,
    rel_recv,
    *buffers,
):
    rels, slots, blocks, z_count, piece, width = sizes
    half = piece // 2
    per = rels * ORDERS
    gathered = buffers[:per]
    pair_out = buffers[per : 2 * per]
    pair_in = buffers[2 * per : 3 * per]
    ring_out = buffers[3 * per : 4 * per]
    ring_in = buffers[4 * per :]

    rel = lax.axis_index("rel")
    row = lax.axis_index("row")
    col = lax.axis_index("col")
    y, x = row // X_CHIPS, row % X_CHIPS
    z, core = col // 2, col % 2

    def row_peer(dy, dx):
        return ((y + dy) % Y_LOW) * X_CHIPS + (x + dx) % X_CHIPS

    def col_peer(dz):
        return ((z + dz) % z_count) * 2 + core

    partner = z * 2 + (1 - core)
    other_rel = 1 - rel

    loads = [
        pltpu.make_async_copy(tiles.at[l], tiles_v.at[l], load_sem.at[l]) for l in range(rels)
    ]
    for load in loads:
        load.start()

    barrier = pltpu.get_barrier_semaphore()
    for dy, dx in ROW_OFFSETS:
        pl.semaphore_signal(barrier, inc=1, device_id={"row": row_peer(dy, dx)}, device_id_type=MESH)
    for other in (partner, col_peer(1), col_peer(-1)):
        pl.semaphore_signal(barrier, inc=1, device_id={"col": other}, device_id_type=MESH)
    pl.semaphore_signal(barrier, inc=1, device_id={"rel": other_rel}, device_id_type=MESH)

    for l in range(rels):
        start = feats[l]
        hist[l, 0] = start
        emb[l] = coefs[l, 0] * start
        gathered[l * ORDERS][row] = start.astype(jnp.bfloat16)
        prefix[l, slots] = jnp.zeros((piece, width), jnp.float32)
    pl.semaphore_wait(barrier, len(ROW_OFFSETS) + 4)

    sends = []

    def send(copy):
        copy.start()
        sends.append(copy)

    def row_copy(l, k, n, source_row, target):
        buffer = gathered[l * ORDERS + k]
        return pltpu.make_async_remote_copy(
            src_ref=buffer.at[source_row],
            dst_ref=buffer.at[source_row],
            send_sem=row_send.at[l, k, n],
            recv_sem=row_recv.at[l, k, n],
            device_id={"row": target},
            device_id_type=MESH,
        )

    def gather_start(l, k):
        for n, (dy, dx) in enumerate(ROW_OFFSETS):
            send(row_copy(l, k, n, row, row_peer(dy, dx)))

    def gather_wait(l, k):
        for n, (dy, dx) in enumerate(ROW_OFFSETS):
            origin = row_peer(-dy, -dx)
            row_copy(l, k, n, origin, row_peer(dy, dx)).wait_recv()

    def pair_copy(l, k, n):
        at = l * ORDERS + k
        return pltpu.make_async_remote_copy(
            src_ref=pair_out[at].at[n],
            dst_ref=pair_in[at].at[n],
            send_sem=pair_send.at[l, k, n],
            recv_sem=pair_recv.at[l, k, n],
            device_id={"col": partner},
            device_id_type=MESH,
        )

    def multiply(l, k):
        source = gathered[l * ORDERS + k]

        def advance(s, carry):
            product = jnp.dot(
                tiles_v[l, s], source[cols[l, s]], preferred_element_type=jnp.float32
            )
            prefix[l, s] = product + prefix[l, before[l, s]]
            return carry

        lax.fori_loop(0, slots, advance, 0, unroll=4)

    def pair_start(l, k):
        for n, delta in enumerate(DELTAS):
            block = ((z + delta) % z_count) * 2 + (1 - core)
            pair_out[l * ORDERS + k][n] = prefix[l, final[l, block]].astype(jnp.bfloat16)
            send(pair_copy(l, k, n))

    def share(l, k, n, lo, size):
        block = ((z + DELTAS[n]) % z_count) * 2 + core
        own = prefix[l, final[l, block], lo : lo + size]
        return own + pair_in[l * ORDERS + k][n, lo : lo + size].astype(jnp.float32)

    def ring_copy(l, k, side, t, h):
        at = l * ORDERS + k
        return pltpu.make_async_remote_copy(
            src_ref=ring_out[at].at[side, t, pl.ds(h * half, half)],
            dst_ref=ring_in[at].at[side, t, pl.ds(h * half, half)],
            send_sem=ring_send.at[l, k, side, t, h],
            recv_sem=ring_recv.at[l, k, side, t, h],
            device_id={"col": col_peer(1 - 2 * side)},
            device_id_type=MESH,
        )

    def ring_step(l, k, t):
        at = l * ORDERS + k
        numbers = [0, 0] if t == 0 else [2 * t - 1, 2 * t]
        for n in sorted(set(numbers)):
            pair_copy(l, k, n).wait_recv()
        for late in (0, 1):
            if t == 0 and late:
                continue
            for side in (0, 1):
                h = side ^ late
                lo = h * half
                value = share(l, k, numbers[side], lo, half)
                if t > late:
                    ring_copy(l, k, side, t - 1, h).wait_recv()
                    value = value + ring_in[at][side, t - 1, lo : lo + half].astype(jnp.float32)
                ring_out[at][side, t, lo : lo + half] = value.astype(jnp.bfloat16)
                send(ring_copy(l, k, side, t, h))

    def finish(l, k):
        at = l * ORDERS + k
        last = len(DELTAS) - 1
        pair_copy(l, k, last).wait_recv()
        for side in (0, 1):
            for h in (0, 1):
                ring_copy(l, k, side, 3, h).wait_recv()
        applied = (
            share(l, k, last, 0, piece)
            + ring_in[at][0, 3].astype(jnp.float32)
            + ring_in[at][1, 3].astype(jnp.float32)
        )
        if k == 0:
            following = applied
        else:
            following = 2.0 * applied - hist[l, (k + 1) % 2]
        if k + 1 < ORDERS:
            gathered[at + 1][row] = following.astype(jnp.bfloat16)
            gather_start(l, k + 1)
            hist[l, (k + 1) % 2] = following
            emb[l] = emb[l] + coefs[l, k + 1] * following
        else:
            emb_send[l] = (emb[l] + coefs[l, k + 1] * following).astype(jnp.bfloat16)
            send(rel_copy(l))

    def rel_copy(l):
        there = pl.ds(pl.multiple_of(other_rel * half, half), half)
        return pltpu.make_async_remote_copy(
            src_ref=emb_send.at[l, there],
            dst_ref=emb_recv.at[l],
            send_sem=rel_send.at[l],
            recv_sem=rel_recv.at[l],
            device_id={"rel": other_rel},
            device_id_type=MESH,
        )

    for l in range(rels):
        gather_start(l, 0)

    for l in range(rels):
        live = count[l]

        def fill_before(s, carry, l=l, live=live):
            mine = rows[l, s]
            prev = jnp.int32(slots)
            for t in range(slots):
                same = (rows[l, t] == mine) & (t < s) & (t < live)
                prev = jnp.where(same, jnp.int32(t), prev)
            before[l, s] = prev
            return carry

        def fill_final(b, carry, l=l, live=live):
            last = jnp.int32(slots)
            for t in range(slots):
                same = (rows[l, t] == b) & (t < live)
                last = jnp.where(same, jnp.int32(t), last)
            final[l, b] = last
            return carry

        lax.fori_loop(0, slots, fill_before, 0)
        lax.fori_loop(0, blocks, fill_final, 0)

    def product(l, k):
        gather_wait(l, k)
        if k == 0:
            loads[l].wait()
        multiply(l, k)
        pair_start(l, k)

    work = [(l, k) for k in range(ORDERS) for l in range(rels)]
    product(*work[0])
    for index, (l, k) in enumerate(work):
        for t in range(4):
            ring_step(l, k, t)
            if t == MIDDLE - 1 and index + 1 < len(work):
                product(*work[index + 1])
        finish(l, k)

    total = jnp.zeros((half, width), jnp.float32)
    here = pl.ds(pl.multiple_of(rel * half, half), half)
    for l in range(rels):
        own_rows = pl.ds(pl.multiple_of((rel * rels + l) * width, width), width)
        total = total + jnp.dot(
            emb_send[l, here], weight[own_rows], preferred_element_type=jnp.float32
        )
    for l in range(rels):
        rel_copy(l).wait_recv()
        far_rows = pl.ds(pl.multiple_of((other_rel * rels + l) * width, width), width)
        total = total + jnp.dot(
            emb_recv[l], weight[far_rows], preferred_element_type=jnp.float32
        )
    out[...] = total
    for copy in sends:
        copy.wait_send()


def local(features, lap_tiles, tile_rows, tile_cols, tile_count, cheb_coefs, merging_weight):
    rels, _, piece, width = features.shape
    slots, side = lap_tiles.shape[3], lap_tiles.shape[4]
    row_count, blocks = lax.axis_size("row"), lax.axis_size("col")
    z_count = blocks // 2
    sizes = (rels, slots, blocks, z_count, piece, width)
    half = piece // 2
    per = rels * ORDERS
    vmem = functools.partial(pltpu.VMEM, dtype=jnp.bfloat16)
    dma = pltpu.SemaphoreType.DMA
    smem = pl.BlockSpec(memory_space=pltpu.SMEM)
    dense = pl.BlockSpec(memory_space=pltpu.VMEM)
    merged = pl.pallas_call(
        functools.partial(kernel, sizes),
        out_shape=jax.ShapeDtypeStruct((half, width), jnp.float32),
        in_specs=[dense, pl.BlockSpec(memory_space=pltpu.HBM), smem, smem, smem, smem, dense],
        out_specs=dense,
        scratch_shapes=[
            vmem((rels, slots, side, side)),
            pltpu.VMEM((rels, slots + 1, piece, width), jnp.float32),
            pltpu.SMEM((rels, slots), jnp.int32),
            pltpu.SMEM((rels, blocks), jnp.int32),
            pltpu.VMEM((rels, 2, piece, width), jnp.float32),
            pltpu.VMEM((rels, piece, width), jnp.float32),
            vmem((rels, piece, width)),
            vmem((rels, half, width)),
            dma((rels,)),
            dma((rels, ORDERS, row_count - 1)),
            dma((rels, ORDERS, row_count - 1)),
            dma((rels, ORDERS, z_count)),
            dma((rels, ORDERS, z_count)),
            dma((rels, ORDERS, 2, 4, 2)),
            dma((rels, ORDERS, 2, 4, 2)),
            dma((rels,)),
            dma((rels,)),
        ]
        + [vmem((row_count, piece, width))] * per
        + [vmem((z_count, piece, width))] * (2 * per)
        + [vmem((2, 4, piece, width))] * (2 * per),
        compiler_params=pltpu.CompilerParams(
            collective_id=0, has_side_effects=True, vmem_limit_bytes=56 * 1024 * 1024
        ),
    )(
        features[:, 0],
        lap_tiles[:, 0, 0],
        tile_rows[:, 0, 0],
        tile_cols[:, 0, 0],
        tile_count[:, 0, 0],
        cheb_coefs,
        merging_weight,
    )
    return merged[None]


def solution(mesh):
    placed = (
        P("rel", ("row", "col"), None, None),
        P("rel", "row", "col", None, None, None),
        P("rel", "row", "col", None),
        P("rel", "row", "col", None),
        P("rel", "row", "col"),
        P("rel", None),
        P(),
    )
    return jax.shard_map(
        local, mesh=mesh, in_specs=placed, out_specs=P(("row", "col"), "rel", None), check_vma=False
    )
```

time: 820 us -> 148 us (0.18)
  the two profiles are of different devices: /device:TPU:1 before, /device:TPU:32 now
where the time goes in v1:
time: 148 us
  Pallas kernels  146 us (99%)
    pallas_call x1, Pallas kernels, local(): pl.pallas_call(functools.partial(kernel, sizes), out_shape=jax.ShapeDtype...  146 us

profile of v1, /device:TPU:32, one launch (start us, length us, event | category | flops | bytes accessed | tf_op | source)
XLA Modules:
  0.0 147.8 jit_solution(14305758894844677443)
XLA Ops:
  0.0 146.3 %shard_map.73 = f32[128,128]{1,0:T(8,128)} custom-call(f32[2,256,128]{2,1,0:T(8,128)} %bitcast.8, bf16[2,16,256,256]{3,2,1,0:T(8,128)(2,1)} %bitcast.6, s32[2,16]{1,0:T(2,128)} %bitcast.9, s32[2,16]{1,0:T(2,128)} %bitcast.10, s32[2]{0:T(128)} %bitcast.11, f32[2,5]{1,0:T(2,128)} %coefs.1, bf16[512,128]{1,0:T(8,128)(2,1)} %weight.1), custom_call_target="tpu_custom_call" | custom-call | tf_op jit(solution)/shard_map/pallas_call | solution.py:290
  146.4 1.5 copy.9

commit v2 on v0

v2 whole, which is shorter than its diff:
```python
import functools

import jax
import jax.numpy as jnp
from jax import lax
from jax.experimental import pallas as pl
from jax.experimental.pallas import tpu as pltpu
from jax.sharding import PartitionSpec as P

ORDERS = 4
X_CHIPS = 4
Y_LOW = 2
MESH = pl.DeviceIdType.MESH
ROW_OFFSETS = ((1, 2), (1, 1), (1, 3), (0, 2), (1, 0), (0, 1), (0, 3), (0, 0))
DELTAS = (3, -3, 4, 2, -2, 1, -1, 0)
ENDS = (0, 1)
HALVES = (0, 1)
SIDES = (0, 1)
UNROLL = 8


def kernel(
    sizes,
    feats,
    tiles,
    table,
    table_out,
    coefs,
    weight,
    out,
    tiles_v,
    far_table,
    prefix,
    sources,
    before,
    final,
    hist,
    emb,
    emb_send,
    emb_recv,
    emb_own,
    start_sem,
    tile_sem,
    tile_send,
    tile_recv,
    table_sems,
    hist_send,
    hist_recv,
    row_send,
    row_recv,
    sum_send,
    sum_recv,
    relay_send,
    relay_recv,
    rel_send,
    rel_recv,
    *buffers,
):
    rels, slots, blocks, z_count, piece, width = sizes
    half = piece // 2
    per = rels * ORDERS
    gathered = buffers[: 2 * per]
    operand = buffers[2 * per : 3 * per]
    sums_out = buffers[3 * per : 4 * per]
    sums_in = buffers[4 * per : 5 * per]
    relay_out = buffers[5 * per : 6 * per]
    relay_in = buffers[6 * per :]
    f32, bf16 = jnp.float32, jnp.bfloat16

    rel = lax.axis_index("rel")
    row = lax.axis_index("row")
    col = lax.axis_index("col")
    y, x = row // X_CHIPS, row % X_CHIPS
    z, core = col // 2, col % 2
    other_rel = 1 - rel
    comm = core == 1
    comp = core == 0

    row_peers = {
        (dy, dx): ((y + dy) % Y_LOW) * X_CHIPS + (x + dx) % X_CHIPS
        for dy in (-1, 0, 1)
        for dx in range(-3, 4)
    }
    chips = {dz: (z + dz) % z_count for dz in range(-4, 5)}

    def row_peer(dy, dx):
        return row_peers[dy, dx]

    def ring_peer(dz, end):
        return chips[dz] * 2 + end

    def at_device(rel=rel, row=row, col=col):
        return (rel, row, col)

    def remote(src, dst, send_sem, recv_sem, **device):
        return pltpu.make_async_remote_copy(
            src_ref=src,
            dst_ref=dst,
            send_sem=send_sem,
            recv_sem=recv_sem,
            device_id=at_device(**device),
            device_id_type=MESH,
        )

    started = {"comm": [], "comp": []}

    def send(who, make, *args):
        make(*args).start()
        started[who].append((make, args))

    def tile_load(l):
        return pltpu.make_async_copy(tiles.at[l], tiles_v.at[l, 0], tile_sem.at[l])

    def tile_copy(l):
        return remote(
            tiles.at[l], tiles_v.at[l, 1], tile_send.at[l], tile_recv.at[l], col=ring_peer(0, 0)
        )

    def table_copy():
        return remote(
            table_out, far_table, table_sems.at[0], table_sems.at[1], col=ring_peer(0, 0)
        )

    def feature_load(l):
        return pltpu.make_async_copy(feats.at[l], hist.at[l, 0, 1], start_sem.at[l])

    def hist_copy(l):
        return remote(
            feats.at[l], hist.at[l, 0, 0], hist_send.at[l], hist_recv.at[l], col=ring_peer(0, 1)
        )

    def rows_of(h):
        return pl.ds(h * half, half)

    def row_copy(l, k, end, h, n, source_row, target):
        at = l * ORDERS + k
        return remote(
            operand[at].at[end, rows_of(h)],
            gathered[2 * at + end].at[source_row].at[rows_of(h)],
            row_send.at[l, k, end, h, n],
            row_recv.at[l, k, end, h, n],
            row=target,
            col=ring_peer(0, 0),
        )

    def sum_copy(l, k, n, end, h):
        at, dz = l * ORDERS + k, DELTAS[n]
        hops = {3: 1, -3: -1, 4: 2 - 4 * end, 2: 0, -2: 0, 1: 1, -1: -1, 0: 0}[dz]
        return remote(
            sums_out[at].at[n, end, rows_of(h)],
            sums_in[at].at[n, end, rows_of(h)],
            sum_send.at[l, k, n, end, h],
            sum_recv.at[l, k, n, end, h],
            col=ring_peer(hops, 1),
        )

    def relay_copy(l, k, side, end, h):
        at = l * ORDERS + k
        return remote(
            relay_out[at].at[side, end, rows_of(h)],
            relay_in[at].at[side, end, rows_of(h)],
            relay_send.at[l, k, side, end, h],
            relay_recv.at[l, k, side, end, h],
            col=ring_peer(2 - 4 * side, 1),
        )

    def rel_copy(l, end):
        there = pl.ds(pl.multiple_of(other_rel * half, half), half)
        return remote(
            emb_send.at[l, end].at[there],
            emb_recv.at[l],
            rel_send.at[l, end],
            rel_recv.at[l, 0],
            rel=other_rel,
            col=ring_peer(0, end),
        )

    def own_copy(l):
        here = pl.ds(pl.multiple_of(rel * half, half), half)
        return remote(
            emb_send.at[l, 0].at[here],
            emb_own.at[l],
            rel_send.at[l, 2],
            rel_recv.at[l, 1],
            col=ring_peer(0, 0),
        )

    barrier = pltpu.get_barrier_semaphore()

    def greet(**device):
        pl.semaphore_signal(barrier, inc=1, device_id=at_device(**device), device_id_type=MESH)

    far_rows = ROW_OFFSETS[:-1]
    for dy, dx in far_rows:
        greet(row=row_peer(dy, dx), col=ring_peer(0, 0))
    greet(rel=other_rel, col=ring_peer(0, 1))
    for dz in (2, -2):
        greet(col=ring_peer(dz, 1))

    @pl.when(comm)
    def _():
        greet(col=ring_peer(0, 0))
        for dz in (2, -2, 1, -1):
            greet(col=ring_peer(dz, 0))
        greet(rel=other_rel, col=ring_peer(0, 0))

    @pl.when(comp)
    def _():
        for dy, dx in far_rows:
            greet(row=row_peer(dy, dx), col=ring_peer(0, 1))
        for dz in (0, 1, -1):
            greet(col=ring_peer(dz, 1))

    for l in range(rels):
        feature_load(l).start()

    @pl.when(comp)
    def _():
        for l in range(rels):
            tile_load(l).start()

    for l in range(rels):
        feature_load(l).wait()
        operand[l * ORDERS][core] = hist[l, 0, 1].astype(bf16)

    @pl.when(comp)
    def _():
        for l in range(rels):
            gathered[2 * l * ORDERS][row] = hist[l, 0, 1].astype(bf16)

    pl.semaphore_wait(barrier, 2 * len(far_rows) + 6 - 4 * core)

    def gather_start(who, l, k, end, h):
        for n, (dy, dx) in enumerate(ROW_OFFSETS if who == "comm" else far_rows):
            send(who, row_copy, l, k, end, h, n, row, row_peer(dy, dx))

    def gather_wait(l, k, end):
        own = k == 0 and end == 0
        for h in HALVES:
            for n, (dy, dx) in enumerate(far_rows if own else ROW_OFFSETS):
                origin = row_peer(-dy, -dx)
                row_copy(l, k, end, h, n, origin, row_peer(dy, dx)).wait_recv()

    @pl.when(comm)
    def _():
        send("comm", table_copy)
        for l in range(rels):
            for h in HALVES:
                gather_start("comm", l, 0, 1, h)
            send("comm", tile_copy, l)

    @pl.when(comp)
    def _():
        for l in range(rels):
            for h in HALVES:
                gather_start("comp", l, 0, 0, h)
        for l in range(rels):
            send("comp", hist_copy, l)

    work = [(l, k) for k in range(ORDERS) for l in range(rels)]

    def fill_tables():
        prefix[2 * slots] = jnp.zeros((piece, width), f32)
        table_copy().wait_recv()
        tables = (table, far_table)
        for l in range(rels):
            base = l * 2 * slots
            lives = [tables[e][rels * 2 * slots + l] for e in ENDS]

            def row_at(e, t, base=base):
                return tables[e][base + t]

            def last_with(mine, below, lives=lives, row_at=row_at):
                found = mine * 0 + 2 * slots
                for e in ENDS:
                    for t in range(slots):
                        same = (row_at(e, t) == mine) & (t < lives[e])
                        if below is not None:
                            same = same & (e * slots + t < below)
                        found = found + same.astype(jnp.int32) * (e * slots + t - found)
                return found

            for e in ENDS:

                def fill_before(s, carry, l=l, e=e, row_at=row_at, last_with=last_with, base=base):
                    sources[l, e * slots + s] = tables[e][base + slots + s]
                    before[l, e * slots + s] = last_with(row_at(e, s), e * slots + s)
                    return carry

                lax.fori_loop(0, slots, fill_before, 0)

            def fill_final(b, carry, l=l, last_with=last_with):
                final[l, b] = last_with(b, None)
                return carry

            lax.fori_loop(0, blocks, fill_final, 0)

    def product(l, k):
        at = l * ORDERS + k
        for end in ENDS:
            gather_wait(l, k, end)
            if k == 0:
                (tile_copy(l).wait_recv if end else tile_load(l).wait)()
            source = gathered[2 * at + end]

            def advance(s, carry, end=end, source=source):
                g = end * slots + s
                value = jnp.dot(
                    tiles_v[l, end, s], source[sources[l, g]], preferred_element_type=f32
                )
                prefix[g] = value + prefix[before[l, g]]
                return carry

            lax.fori_loop(0, slots, advance, 0, unroll=UNROLL)

    def sums_start(l, k):
        at = l * ORDERS + k

        def put(dz, end):
            n = DELTAS.index(dz)
            block = chips[dz] * 2 + end
            for h in HALVES:
                lo = h * half
                value = prefix[final[l, block], lo : lo + half]
                sums_out[at][n, end, lo : lo + half] = value.astype(bf16)
                send("comp", sum_copy, l, k, n, end, h)

        for end in ENDS:
            for dz in (3, -3, 4, 2, -2):
                put(dz, end)
        for end in ENDS:
            for dz in (1, -1, 0):
                put(dz, end)

    def taken(l, k, dz, end, h):
        n, lo = DELTAS.index(dz), h * half
        sum_copy(l, k, n, end, h).wait_recv()
        return sums_in[l * ORDERS + k][n, end, lo : lo + half].astype(f32)

    def relay(l, k):
        at = l * ORDERS + k
        for end in ENDS:
            for h in HALVES:
                for side in SIDES if end else SIDES[::-1]:
                    lo, sign = h * half, 1 - 2 * side
                    value = taken(l, k, 2 * sign, end, h) + taken(l, k, 3 * sign, end, h)
                    if end == side:
                        value = value + taken(l, k, 4, end, h)
                    relay_out[at][side, end, lo : lo + half] = value.astype(bf16)
                    send("comm", relay_copy, l, k, side, end, h)

    def finish(l, k):
        at = l * ORDERS + k
        for end in ENDS:
            for h in HALVES:
                lo = h * half
                part = slice(lo, lo + half)
                value = taken(l, k, 0, end, h) + taken(l, k, 1, end, h) + taken(l, k, -1, end, h)
                for side in SIDES:
                    relay_copy(l, k, side, end, h).wait_recv()
                    value = value + relay_in[at][side, end, part].astype(f32)
                if k > 0:
                    value = 2.0 * value - hist[l, (k + 1) % 2, end, part]
                if k + 1 < ORDERS:
                    operand[at + 1][end, part] = value.astype(bf16)
                    gather_start("comm", l, k + 1, end, h)
                    hist[l, (k + 1) % 2, end, part] = value
                    emb[l, end, part] = emb[l, end, part] + coefs[l, k + 1] * value
                else:
                    total = emb[l, end, part] + coefs[l, k + 1] * value
                    emb_send[l, end, part] = total.astype(bf16)
            if k + 1 == ORDERS:
                send("comm", rel_copy, l, end)
                if end == 0:
                    send("comm", own_copy, l)

    @pl.when(comp)
    def _():
        fill_tables()
        for l, k in work:
            product(l, k)
            sums_start(l, k)

    @pl.when(comm)
    def _():
        for l in range(rels):
            hist_copy(l).wait_recv()
            for end in ENDS:
                emb[l, end] = coefs[l, 0] * hist[l, 0, end]
        for l, k in work:
            relay(l, k)
            finish(l, k)
        here = pl.ds(pl.multiple_of(rel * half, half), half)
        for l in range(rels):
            emb_own[l] = emb_send[l, 1, here]

    @pl.when(comp)
    def _():
        for l in range(rels):
            own_copy(l).wait_recv()

    total = jnp.zeros((half, width), f32)
    for l in range(rels):
        rel_copy(l, 0).wait_recv()
        for side_rel, part in ((rel, emb_own), (other_rel, emb_recv)):
            rows = pl.ds(pl.multiple_of((side_rel * rels + l) * width, width), width)
            total = total + jnp.dot(part[l], weight[rows], preferred_element_type=f32)
    out[...] = total

    for who, active in (("comm", comm), ("comp", comp)):

        @pl.when(active)
        def _(who=who):
            for make, args in started[who]:
                make(*args).wait_send()


def local(features, lap_tiles, tile_rows, tile_cols, tile_count, cheb_coefs, merging_weight):
    rels, _, piece, width = features.shape
    slots, side = lap_tiles.shape[3], lap_tiles.shape[4]
    row_count, blocks = lax.axis_size("row"), lax.axis_size("col")
    z_count = blocks // 2
    sizes = (rels, slots, blocks, z_count, piece, width)
    half = piece // 2
    per = rels * ORDERS
    table = jnp.concatenate([tile_rows[:, 0, 0], tile_cols[:, 0, 0]], axis=1).reshape(-1)
    table = jnp.concatenate([table, tile_count[:, 0, 0]])
    table = jnp.pad(table, (0, -table.shape[0] % 128))
    vmem = functools.partial(pltpu.VMEM, dtype=jnp.bfloat16)
    wide = functools.partial(pltpu.VMEM, dtype=jnp.float32)
    dma = pltpu.SemaphoreType.DMA
    smem = pl.BlockSpec(memory_space=pltpu.SMEM)
    dense = pl.BlockSpec(memory_space=pltpu.VMEM)
    far = pl.BlockSpec(memory_space=pltpu.HBM)
    merged = pl.pallas_call(
        functools.partial(kernel, sizes),
        out_shape=jax.ShapeDtypeStruct((half, width), jnp.float32),
        in_specs=[far, far, smem, far, smem, dense],
        out_specs=dense,
        scratch_shapes=[
            vmem((rels, 2, slots, side, side)),
            pltpu.SMEM(table.shape, jnp.int32),
            wide((2 * slots + 1, piece, width)),
            pltpu.SMEM((rels, 2 * slots), jnp.int32),
            pltpu.SMEM((rels, 2 * slots), jnp.int32),
            pltpu.SMEM((rels, blocks), jnp.int32),
            wide((rels, 2, 2, piece, width)),
            wide((rels, 2, piece, width)),
            vmem((rels, 2, piece, width)),
            vmem((rels, half, width)),
            vmem((rels, half, width)),
            dma((rels,)),
            dma((rels,)),
            dma((rels,)),
            dma((rels,)),
            dma((2,)),
            dma((rels,)),
            dma((rels,)),
            dma((rels, ORDERS, 2, 2, row_count)),
            dma((rels, ORDERS, 2, 2, row_count)),
            dma((rels, ORDERS, z_count, 2, 2)),
            dma((rels, ORDERS, z_count, 2, 2)),
            dma((rels, ORDERS, 2, 2, 2)),
            dma((rels, ORDERS, 2, 2, 2)),
            dma((rels, 3)),
            dma((rels, 2)),
        ]
        + [vmem((row_count, piece, width))] * (2 * per)
        + [vmem((2, piece, width))] * per
        + [vmem((z_count, 2, piece, width))] * (2 * per)
        + [vmem((2, 2, piece, width))] * (2 * per),
        compiler_params=pltpu.CompilerParams(
            collective_id=0, has_side_effects=True, vmem_limit_bytes=62 * 1024 * 1024
        ),
    )(
        features[:, 0],
        lap_tiles[:, 0, 0],
        table,
        table,
        cheb_coefs,
        merging_weight,
    )
    return merged[None]


def solution(mesh):
    placed = (
        P("rel", ("row", "col"), None, None),
        P("rel", "row", "col", None, None, None),
        P("rel", "row", "col", None),
        P("rel", "row", "col", None),
        P("rel", "row", "col"),
        P("rel", None),
        P(),
    )
    return jax.shard_map(
        local, mesh=mesh, in_specs=placed, out_specs=P(("row", "col"), "rel", None), check_vma=False
    )
```

time: 820 us -> 112 us (0.14); the launches traced: 811 us -> 112 us
  starting transfers between devices: 389 us -> 0 us
  waiting for transfers between devices: 221 us -> 0 us
  Pallas kernels: 0 us -> 108 us
  loops' own time: 81.7 us -> 0 us
  local copies, waits for them, and re-layouts: 63.9 us -> 2.07 us
  matrix products: 44.3 us -> 0 us
  other arithmetic: 11.3 us -> 1.5 us
    all_to_all x17 -> x0, starting transfers between devices: 389 us -> none  [the longest x8 342 us: sum_at_owner(): lax.all_to_all(pieces, axis, split_axis=0, concat_axis=0, tiled=True)]
    all_to_all x17 -> x0, waiting for transfers between devices: 221 us -> none  [the longest x8 182 us: sum_at_owner(): lax.all_to_all(pieces, axis, split_axis=0, concat_axis=0, tiled=True)]
    pallas_call x0 -> x1, Pallas kernels: none -> 108 us  [local(): pl.pallas_call(functools.partial(kernel, sizes), out_shape=jax.ShapeDtype...]
    another operation x8 -> x0, loops' own time: 81.7 us -> none  [local_product(): running = lax.fori_loop(0, block_count, advance, running)]
    dynamic_slice x80 -> x0, local copies, waits for them, and re-layouts: 49.1 us -> none  [the longest x40 24.6 us: advance(): start_row = block_rows[slot_index] * tile_size]
    dot_general x42 -> x0, matrix products: 44.3 us -> none  [the longest x40 43.3 us: advance(): jnp.dot(block_tile, source_rows, preferred_element_type=jnp.float32)]
    convert_element_type x13 -> x0, other arithmetic: 10.2 us -> none  [the longest x8 8.92 us: local(): collected.append(sum_at_owner(partial_value.astype(jnp.bfloat16), 'col', 0))]
  transfers between devices with their start and end apart: 17 -> 0, of which waited for: 13 -> 0; matrix products, arithmetic and copies ran while one was open for 13% -> 0% of each run, Pallas kernels for 0% -> 0%
where the time goes in v2:
time: 112 us
  Pallas kernels  108 us (96%)
  local copies, waits for them, and re-layouts  2.07 us (2%)
  other arithmetic  1.5 us (1%)
    pallas_call x1, Pallas kernels, local(): pl.pallas_call(functools.partial(kernel, sizes), out_shape=jax.ShapeDtype...  108 us

profile of v2, /device:TPU:1, one launch (start us, length us, event | category | flops | bytes accessed | tf_op | source)
XLA Modules:
  0.0 111.6 jit_solution(4835616988793973735)
XLA Ops:
  0.0 0.8 pad_add_fusion
  0.8 0.1 reshape.3
  0.9 0.7 pad_add_fusion.1
  1.6 0.5 pad.4.table.table_out
  2.1 108.0 %shard_map.73 = f32[128,128]{1,0:T(8,128)} custom-call(f32[2,256,128]{2,1,0:T(8,128)} %bitcast.8, bf16[2,16,256,256]{3,2,1,0:T(8,128)(2,1)} %bitcast.6, s32[128]{0:T(128)} %pad.4.table.table_out, s32[128]{0:T(128)} %pad.4.table.table_out, f32[2,5]{1,0:T(2,128)} %coefs.1, bf16[512,128]{1,0:T(8,128)(2,1)} %weight.1), custom_call_target="tpu_custom_call" | custom-call | tf_op jit(solution)/shard_map/pallas_call | solution.py:435
  110.1 1.5 %copy.9 = f32[1,128,128]{2,1,0:T(8,128)} copy(f32[1,128,128]{2,1,0:T(8,128)} %bitcast.7) | data formatting | bytes 131072

commit v3 on v2

--- a/solution.py
+++ b/solution.py
@@ -16,20 +16,28 @@
 ENDS = (0, 1)
 HALVES = (0, 1)
 SIDES = (0, 1)
-UNROLL = 8
+UNROLL = 16
 
 
 def kernel(
     sizes,
     feats,
     tiles,
-    table,
-    table_out,
+    tile_rows,
+    tile_cols,
+    tile_count,
+    cheb_coefs,
+    merging_weight,
+    out,
+    tiles_v,
+    rows_0,
+    rows_1,
+    cols_0,
+    cols_1,
+    count_0,
+    count_1,
     coefs,
     weight,
-    out,
-    tiles_v,
-    far_table,
     prefix,
     sources,
     before,
@@ -43,7 +51,10 @@
     tile_sem,
     tile_send,
     tile_recv,
-    table_sems,
+    table_load,
+    table_send,
+    table_recv,
+    late_sem,
     hist_send,
     hist_recv,
     row_send,
@@ -116,10 +127,20 @@
             tiles.at[l], tiles_v.at[l, 1], tile_send.at[l], tile_recv.at[l], col=ring_peer(0, 0)
         )
 
-    def table_copy():
-        return remote(
-            table_out, far_table, table_sems.at[0], table_sems.at[1], col=ring_peer(0, 0)
-        )
+    near_tables = ((tile_rows, rows_0), (tile_cols, cols_0), (tile_count, count_0))
+    far_tables = ((tile_rows, rows_1), (tile_cols, cols_1), (tile_count, count_1))
+
+    def table_near(i):
+        return pltpu.make_async_copy(*near_tables[i], table_load.at[i])
+
+    def table_copy(i):
+        src, dst = far_tables[i]
+        return remote(src, dst, table_send.at[i], table_recv.at[i], col=ring_peer(0, 0))
+
+    late_loads = [
+        pltpu.make_async_copy(cheb_coefs, coefs, late_sem.at[0]),
+        pltpu.make_async_copy(merging_weight, weight, late_sem.at[1]),
+    ]
 
     def feature_load(l):
         return pltpu.make_async_copy(feats.at[l], hist.at[l, 0, 1], start_sem.at[l])
@@ -216,6 +237,8 @@
 
     @pl.when(comp)
     def _():
+        for i in range(3):
+            table_near(i).start()
         for l in range(rels):
             tile_load(l).start()
 
@@ -228,6 +251,8 @@
         for l in range(rels):
             gathered[2 * l * ORDERS][row] = hist[l, 0, 1].astype(bf16)
 
+    for load in late_loads:
+        load.start()
     pl.semaphore_wait(barrier, 2 * len(far_rows) + 6 - 4 * core)
 
     def gather_start(who, l, k, end, h):
@@ -243,7 +268,8 @@
 
     @pl.when(comm)
     def _():
-        send("comm", table_copy)
+        for i in range(3):
+            send("comm", table_copy, i)
         for l in range(rels):
             for h in HALVES:
                 gather_start("comm", l, 0, 1, h)
@@ -261,39 +287,34 @@
 
     def fill_tables():
         prefix[2 * slots] = jnp.zeros((piece, width), f32)
-        table_copy().wait_recv()
-        tables = (table, far_table)
-        for l in range(rels):
-            base = l * 2 * slots
-            lives = [tables[e][rels * 2 * slots + l] for e in ENDS]
-
-            def row_at(e, t, base=base):
-                return tables[e][base + t]
-
-            def last_with(mine, below, lives=lives, row_at=row_at):
-                found = mine * 0 + 2 * slots
-                for e in ENDS:
-                    for t in range(slots):
-                        same = (row_at(e, t) == mine) & (t < lives[e])
-                        if below is not None:
-                            same = same & (e * slots + t < below)
-                        found = found + same.astype(jnp.int32) * (e * slots + t - found)
-                return found
-
-            for e in ENDS:
-
-                def fill_before(s, carry, l=l, e=e, row_at=row_at, last_with=last_with, base=base):
-                    sources[l, e * slots + s] = tables[e][base + slots + s]
-                    before[l, e * slots + s] = last_with(row_at(e, s), e * slots + s)
-                    return carry
-
-                lax.fori_loop(0, slots, fill_before, 0)
-
-            def fill_final(b, carry, l=l, last_with=last_with):
-                final[l, b] = last_with(b, None)
-                return carry
-
-            lax.fori_loop(0, blocks, fill_final, 0)
+        for i in range(3):
+            table_near(i).wait()
+        for i in range(3):
+            table_copy(i).wait_recv()
+        for l in range(rels):
+            none = count_0[l] * 0 + 2 * slots
+            lasts = (none,) * blocks
+            for e, (rows_e, cols_e, count_e) in enumerate(
+                ((rows_0, cols_0, count_0), (rows_1, cols_1, count_1))
+            ):
+                live = count_e[l]
+
+                def fill(s, lasts, l=l, e=e, rows_e=rows_e, cols_e=cols_e, live=live, none=none):
+                    g = e * slots + s
+                    mine = rows_e[l, s]
+                    found = none
+                    after = []
+                    for b in range(blocks):
+                        hit = mine == b
+                        found = jnp.where(hit, lasts[b], found)
+                        after.append(jnp.where(hit & (s < live), g, lasts[b]))
+                    sources[l, g] = cols_e[l, s]
+                    before[l, g] = found
+                    return tuple(after)
+
+                lasts = lax.fori_loop(0, slots, fill, lasts)
+            for b in range(blocks):
+                final[l, b] = lasts[b]
 
     def product(l, k):
         at = l * ORDERS + k
@@ -316,21 +337,18 @@
     def sums_start(l, k):
         at = l * ORDERS + k
 
-        def put(dz, end):
-            n = DELTAS.index(dz)
+        def put(dz, end, h):
+            n, lo = DELTAS.index(dz), h * half
             block = chips[dz] * 2 + end
-            for h in HALVES:
-                lo = h * half
-                value = prefix[final[l, block], lo : lo + half]
-                sums_out[at][n, end, lo : lo + half] = value.astype(bf16)
-                send("comp", sum_copy, l, k, n, end, h)
-
-        for end in ENDS:
-            for dz in (3, -3, 4, 2, -2):
-                put(dz, end)
-        for end in ENDS:
-            for dz in (1, -1, 0):
-                put(dz, end)
+            value = prefix[final[l, block], lo : lo + half]
+            sums_out[at][n, end, lo : lo + half] = value.astype(bf16)
+            send("comp", sum_copy, l, k, n, end, h)
+
+        for hops in ((3, -3, 4, 2, -2), (1, -1, 0)):
+            for end in ENDS:
+                for h in HALVES:
+                    for dz in hops:
+                        put(dz, end, h)
 
     def taken(l, k, dz, end, h):
         n, lo = DELTAS.index(dz), h * half
@@ -385,6 +403,8 @@
     def _():
         for l in range(rels):
             hist_copy(l).wait_recv()
+            if l == 0:
+                late_loads[0].wait()
             for end in ENDS:
                 emb[l, end] = coefs[l, 0] * hist[l, 0, end]
         for l, k in work:
@@ -398,13 +418,20 @@
     def _():
         for l in range(rels):
             own_copy(l).wait_recv()
-
+        late_loads[0].wait()
+
+    late_loads[1].wait()
     total = jnp.zeros((half, width), f32)
+
+    def merged(part, l, side_rel):
+        rows = pl.ds(pl.multiple_of((side_rel * rels + l) * width, width), width)
+        return jnp.dot(part[l], weight[rows], preferred_element_type=f32)
+
+    for l in range(rels):
+        total = total + merged(emb_own, l, rel)
     for l in range(rels):
         rel_copy(l, 0).wait_recv()
-        for side_rel, part in ((rel, emb_own), (other_rel, emb_recv)):
-            rows = pl.ds(pl.multiple_of((side_rel * rels + l) * width, width), width)
-            total = total + jnp.dot(part[l], weight[rows], preferred_element_type=f32)
+        total = total + merged(emb_recv, l, other_rel)
     out[...] = total
 
     for who, active in (("comm", comm), ("comp", comp)):
@@ -423,23 +450,26 @@
     sizes = (rels, slots, blocks, z_count, piece, width)
     half = piece // 2
     per = rels * ORDERS
-    table = jnp.concatenate([tile_rows[:, 0, 0], tile_cols[:, 0, 0]], axis=1).reshape(-1)
-    table = jnp.concatenate([table, tile_count[:, 0, 0]])
-    table = jnp.pad(table, (0, -table.shape[0] % 128))
     vmem = functools.partial(pltpu.VMEM, dtype=jnp.bfloat16)
     wide = functools.partial(pltpu.VMEM, dtype=jnp.float32)
     dma = pltpu.SemaphoreType.DMA
-    smem = pl.BlockSpec(memory_space=pltpu.SMEM)
     dense = pl.BlockSpec(memory_space=pltpu.VMEM)
     far = pl.BlockSpec(memory_space=pltpu.HBM)
     merged = pl.pallas_call(
         functools.partial(kernel, sizes),
         out_shape=jax.ShapeDtypeStruct((half, width), jnp.float32),
-        in_specs=[far, far, smem, far, smem, dense],
+        in_specs=[far] * 7,
         out_specs=dense,
         scratch_shapes=[
             vmem((rels, 2, slots, side, side)),
-            pltpu.SMEM(table.shape, jnp.int32),
+            pltpu.SMEM((rels, slots), jnp.int32),
+            pltpu.SMEM((rels, slots), jnp.int32),
+            pltpu.SMEM((rels, slots), jnp.int32),
+            pltpu.SMEM((rels, slots), jnp.int32),
+            pltpu.SMEM((rels,), jnp.int32),
+            pltpu.SMEM((rels,), jnp.int32),
+            pltpu.SMEM(cheb_coefs.shape, jnp.float32),
+            vmem(merging_weight.shape),
             wide((2 * slots + 1, piece, width)),
             pltpu.SMEM((rels, 2 * slots), jnp.int32),
             pltpu.SMEM((rels, 2 * slots), jnp.int32),
@@ -453,6 +483,9 @@
             dma((rels,)),
             dma((rels,)),
             dma((rels,)),
+            dma((3,)),
+            dma((3,)),
+            dma((3,)),
             dma((2,)),
             dma((rels,)),
             dma((rels,)),
@@ -475,8 +508,9 @@
     )(
         features[:, 0],
         lap_tiles[:, 0, 0],
-        table,
-        table,
+        tile_rows[:, 0, 0],
+        tile_cols[:, 0, 0],
+        tile_count[:, 0, 0],
         cheb_coefs,
         merging_weight,
     )

time: 112 us -> 104 us (0.929)
  Pallas kernels: 108 us -> 103 us
  other arithmetic: 1.5 us -> 0 us
    pallas_call x1, Pallas kernels: 108 us -> 103 us  [local(): pl.pallas_call(functools.partial(kernel, sizes), out_shape=jax.ShapeDtype...]
    concatenate x2 -> x0, other arithmetic: 1.5 us -> none  [the longest x1 0.77 us: local(): jnp.concatenate([tile_rows[:, 0, 0], tile_cols[:, 0, 0]], axis=1)]
where the time goes in v3:
time: 104 us
  Pallas kernels  103 us (99%)
  local copies, waits for them, and re-layouts  1.47 us (1%)
    pallas_call x1, Pallas kernels, local(): pl.pallas_call(functools.partial(kernel, sizes), out_shape=jax.ShapeDtype...  103 us

profile of v3, /device:TPU:1, one launch (start us, length us, event | category | flops | bytes accessed | tf_op | source)
XLA Modules:
  0.0 104.3 jit_solution(17556383298667885838)
XLA Ops:
  0.0 102.8 %shard_map.73 = f32[128,128]{1,0:T(8,128)} custom-call(f32[2,256,128]{2,1,0:T(8,128)} %bitcast.8, bf16[2,16,256,256]{3,2,1,0:T(8,128)(2,1)} %bitcast.6, s32[2,16]{1,0:T(2,128)} %bitcast.9, s32[2,16]{1,0:T(2,128)} %bitcast.10, s32[2]{0:T(128)} %bitcast.11, f32[2,5]{1,0:T(2,128)} %cheb_coefs.1, bf16[512,128]{1,0:T(8,128)(2,1)} %merging_weight.1), custom_call_target="tpu_custom_call" | custom-call | tf_op jit(solution)/shard_map/pallas_call | solution.py:458
  102.8 1.5 %copy.9 = f32[1,128,128]{2,1,0:T(8,128)} copy(f32[1,128,128]{2,1,0:T(8,128)} %bitcast.7) | data formatting | bytes 131072
